TPU v7x, 32 devices: a whole 2x2x4 slice. The times are simulated.
32 devices in a mesh: rep: 4 (over z), row: 4 (over x, core), col: 2 (over y).
Axes of the slice: x: 2, y: 2, z: 4, core: 2. Of those that a mesh axis runs over, the one named last changes fastest.
Arguments:
- grad_parts: bfloat16 [4, 16384, 6144], P('rep', ('row', 'col')), may hold values from -0.03125 to 0.03125, as said below
- statistic: float32 [6144, 6144], P('row', 'col'), may hold values from -150 to 150, as said below
Outputs:
- gram_matrix: float32 [6144, 6144], P('row', 'col')
- statistic_next: float32 [6144, 6144], P('row', 'col')
Inputs may be any that keep to these rules, and one draw needn't show every extreme that they name: Every entry of grad_parts has a magnitude between 2^-10 and 2^-5. statistic is symmetric and positive definite.
All inputs are finite; a program needn't handle non-finite values.
Results may differ from a plain program's by a relative error of at most 0.008.
Values may be sent and summed in bfloat16 or wider, within the bound.
A program may use at most 192 MiB of HBM per device.

v0:
```python
import functools

import jax
import jax.numpy as jnp
from jax import lax
from jax.experimental import pallas as pl
from jax.experimental.pallas import tpu as pltpu
from jax.sharding import PartitionSpec as P

ITEMS = 32
MIDDLE = 4
BANDS = 6
PARTS = 2
SLABS = 4
CHUNK = 1536
STRIP = 16
VMEM_LIMIT = 62 * 2**20
MESH = pl.DeviceIdType.MESH


def plan(reps):
    middle = MIDDLE if reps > 2 else 0
    end = (ITEMS - (reps - 2) * middle) // 2
    return end, middle, end + (reps - 2) * middle


def bits_of(axis, size):
    bits, bit = [], size // 2
    while bit:
        bits.append((axis, bit))
        bit //= 2
    return bits


def digit(axis, bit):
    return lax.rem(lax.axis_index(axis) // bit, 2)


def partner(axis, bit):
    return {axis: lax.axis_index(axis) + bit - 2 * bit * digit(axis, bit)}


def greet(bits, reps, others=()):
    here = lax.axis_index("rep")
    barrier = pltpu.get_barrier_semaphore()

    def signal(device):
        pl.semaphore_signal(barrier, inc=1, device_id=device, device_id_type=MESH)

    for axis, bit in bits:
        signal(partner(axis, bit))
    for device in others:
        signal(device)
    pl.when(here > 0)(lambda: signal({"rep": here - 1}))
    pl.when(here < reps - 1)(lambda: signal({"rep": here + 1}))
    ends = jnp.where(here > 0, 1, 0) + jnp.where(here < reps - 1, 1, 0)
    pl.semaphore_wait(barrier, len(bits) + len(others) + ends)


def add_strips(out, *refs):
    rows = out.shape[0]

    def strip(n, carry):
        at = pl.ds(pl.multiple_of(n * STRIP, STRIP), STRIP)
        total = refs[0][at, :].astype(jnp.float32)
        for ref in refs[1:]:
            total = total + ref[at, :].astype(jnp.float32)
        out[at, :] = total.astype(out.dtype)
        return carry

    lax.fori_loop(0, rows // STRIP, strip, 0)


def collect_kernel(
    reps, bits, orders, own, out, ups, downs, loads, zeros,
    load_sem, up_send, up_recv, down_send, down_recv, hop_send, hop_recv, keep_sem, zero_sem,
):
    end, middle, length = plan(reps)
    here = lax.axis_index("rep")
    mirror = reps - 1 - here
    at_end = (here == 0) | (here == reps - 1)
    inside = (here > 0) & (here < reps - 1)
    size, width = loads.shape[1], loads.shape[2]
    half = width // 2
    kept = jnp.where(at_end, end, middle)
    base = jnp.where(at_end, reps - 1, end + middle + 1)

    greet(bits, reps)

    def rows(position):
        return own.at[pl.ds(pl.multiple_of(position * size, size), size), :]

    def load(slot, position):
        return pltpu.make_async_copy(rows(position), loads.at[slot], load_sem.at[slot])

    def chain(slots, send, recv, j, to, source=None):
        return pltpu.make_async_remote_copy(
            src_ref=slots.at[j] if source is None else source,
            dst_ref=slots.at[j],
            send_sem=send.at[j],
            recv_sem=recv.at[j],
            device_id={"rep": to},
            device_id_type=MESH,
        )

    def go_up(j, source=None):
        return chain(ups, up_send, up_recv, j, here + 1, source)

    def go_down(j, source=None):
        return chain(downs, down_send, down_recv, j, here - 1, source)

    def up_items(place):
        return jnp.where(place < reps - 1, end + (reps - 2 - place) * middle, 0)

    def place_of(f, exchanged, h):
        index = [f]
        for axis, bit in bits:
            index.append(slice(None) if (axis, bit) in exchanged else digit(axis, bit))
        index.append(slice(None))
        index.append(pl.ds(h * half, half))
        return out.at[tuple(index)]

    def hop(f, h, stage, source=None):
        order = orders[h]
        spot = place_of(f, order[:stage], h)
        return pltpu.make_async_remote_copy(
            src_ref=spot if source is None else source,
            dst_ref=spot,
            send_sem=hop_send.at[f, h, stage],
            recv_sem=hop_recv.at[f, h, stage],
            device_id=partner(*order[stage]),
            device_id_type=MESH,
        )

    def keep(f, source):
        index = tuple([f] + [digit(axis, bit) for axis, bit in bits])
        return pltpu.make_async_copy(source, out.at[index], keep_sem.at[f])

    def spread(f, source):
        for h in range(2):
            hop(f, h, 0, source.at[:, pl.ds(h * half, half)]).start()
        keep(f, source).start()

    spare = end - middle
    if spare:

        @pl.when(inside)
        def _():
            zeros[...] = jnp.zeros_like(zeros)

            def fill(n, carry):
                left, index = n, []
                for _ in bits:
                    index.append(lax.rem(left, 2))
                    left = left // 2
                at = tuple([middle + left] + index)
                pltpu.make_async_copy(zeros, out.at[at], zero_sem).start()
                return carry

            lax.fori_loop(0, spare * 2 ** len(bits), fill, 0)

    stages = len(bits)
    ticks = max(
        length + reps - 2,
        reps + stages + (3 * (end - 1)) // 2,
        (end + middle + 2 + stages + (3 * (middle - 1)) // 2) if middle else 0,
    )

    def tick(t, carry):
        up_j, down_j = t - here, t - mirror
        up_on = (up_j >= 0) & (up_j < up_items(here))
        down_on = (down_j >= 0) & (down_j < up_items(mirror))
        f = t - base
        final_on = (f >= 0) & (f < kept)
        late = here * 2 >= reps
        offset = jnp.where(late, f, middle - 1 - f)
        position = jnp.where(
            here == 0, f, jnp.where(mirror == 0, ITEMS - 1 - f, end + (here - 1) * middle + offset)
        )

        pl.when(up_on & (here > 0))(lambda: load(0, ITEMS - 1 - up_j).start())
        pl.when(down_on & (mirror > 0))(lambda: load(1, down_j).start())
        pl.when(final_on)(lambda: load(2, position).start())

        pl.when(up_on & (here == 0))(lambda: go_up(up_j, rows(ITEMS - 1 - up_j)).start())
        pl.when(down_on & (mirror == 0))(lambda: go_down(down_j, rows(down_j)).start())

        @pl.when(up_on & (here > 0))
        def _():
            load(0, ITEMS - 1 - up_j).wait()
            go_up(up_j).wait_recv()
            slot = ups.at[up_j]
            add_strips(slot, slot, loads.at[0])
            go_up(up_j).start()

        @pl.when(down_on & (mirror > 0))
        def _():
            load(1, down_j).wait()
            go_down(down_j).wait_recv()
            slot = downs.at[down_j]
            add_strips(slot, slot, loads.at[1])
            go_down(down_j).start()

        @pl.when(final_on & (here == 0))
        def _():
            load(2, position).wait()
            go_down(f).wait_recv()
            add_strips(downs.at[f], downs.at[f], loads.at[2])
            spread(f, downs.at[f])

        @pl.when(final_on & (mirror == 0))
        def _():
            load(2, position).wait()
            go_up(f).wait_recv()
            add_strips(ups.at[f], ups.at[f], loads.at[2])
            spread(f, ups.at[f])

        @pl.when(final_on & inside)
        def _():
            load(2, position).wait()
            up, down = ITEMS - 1 - position, position
            go_up(up).wait_recv()
            go_down(down).wait_recv()
            add_strips(ups.at[up], ups.at[up], downs.at[down], loads.at[2])
            spread(f, ups.at[up])

        for stage in range(1, stages + 1):
            m = t - base - stage
            g = 2 * (m // 3) + lax.rem(m, 3)

            @pl.when((m >= 0) & (lax.rem(m, 3) < 2) & (g < kept))
            def _():
                for h in range(2):
                    hop(g, h, stage - 1).wait_recv()
                    hop(g, h, stage - 1).wait_send()
                if stage == 1:
                    keep(g, loads.at[2]).wait()
                if stage < stages:
                    for h in range(2):
                        hop(g, h, stage).start()

        return carry

    lax.fori_loop(0, ticks, tick, 0)

    def drain(j, carry):
        pl.when(j < up_items(here))(lambda: go_up(j).wait_send())
        pl.when(j < up_items(mirror))(lambda: go_down(j).wait_send())
        return carry

    lax.fori_loop(0, length, drain, 0)
    if spare:

        @pl.when(inside)
        def _():
            spot = out.at[pl.ds(middle, spare)]
            pltpu.make_async_copy(spot, spot, zero_sem).wait()


def collect(own):
    reps = lax.axis_size("rep")
    end, middle, length = plan(reps)
    row_bits = bits_of("row", lax.axis_size("row"))
    col_bits = bits_of("col", lax.axis_size("col"))
    bits = row_bits + col_bits
    orders = (col_bits + row_bits, row_bits[:-1] + col_bits + row_bits[-1:])
    size, width = own.shape[0] // ITEMS, own.shape[1]
    dma = pltpu.SemaphoreType.DMA
    gathered = pl.pallas_call(
        functools.partial(collect_kernel, reps, bits, orders),
        out_shape=jax.ShapeDtypeStruct((end,) + (2,) * len(bits) + (size, width), own.dtype),
        in_specs=[pl.BlockSpec(memory_space=pl.ANY)],
        out_specs=pl.BlockSpec(memory_space=pl.ANY),
        scratch_shapes=[
            pltpu.VMEM((length, size, width), own.dtype),
            pltpu.VMEM((length, size, width), own.dtype),
            pltpu.VMEM((3, size, width), own.dtype),
            pltpu.VMEM((size, width), own.dtype),
            dma((3,)),
            dma((length,)),
            dma((length,)),
            dma((length,)),
            dma((length,)),
            dma((end, 2, len(bits))),
            dma((end, 2, len(bits))),
            dma((end,)),
            dma,
        ],
        compiler_params=pltpu.CompilerParams(
            collective_id=0, has_side_effects=True, vmem_limit_bytes=VMEM_LIMIT
        ),
    )(own)
    return gathered.reshape(-1, width)


def total_kernel(
    reps, rows, cols, shared, summed, out, held, ups, downs, sends, left, right, turned,
    left_sem, right_sem, out_sem, up_send, up_recv, down_send, down_recv, *extra,
):
    here = lax.axis_index("rep")
    mirror = reps - 1 - here
    bands, size, band_cols = held.shape
    depth = left.shape[1]
    slabs = summed.shape[0] // depth
    chunk = min(CHUNK, band_cols)
    row, col = lax.axis_index("row"), lax.axis_index("col")
    if shared:
        given, taken, square, pair_send, pair_recv, square_sem = extra
        twin_row = jnp.where(row // 2 == col, row + 1 - 2 * lax.rem(row, 2), 2 * col + lax.rem(row, 2))
        twin = {"row": twin_row, "col": row // 2}
        low = row < twin_row
        twin_place = (twin_row - 2 * col) * rows
        own_place = rows - twin_place
        half = rows // 2
    else:
        own_place = 0

    def starts(k):
        plain = row * rows + (k - shared) * size, col * cols + own_place
        if not shared:
            return plain
        first = jnp.where(low, row * rows, twin_row * rows + half) + k * size
        second = jnp.where(low, twin_row, row) * rows
        is_shared = k < shared
        return jnp.where(is_shared, first, plain[0]), jnp.where(is_shared, second, plain[1])

    def fetch(k, n, slot):
        along = pl.ds(pl.multiple_of(n * depth, depth), depth)
        down, across = starts(k)
        return (
            pltpu.make_async_copy(
                summed.at[along, pl.ds(pl.multiple_of(down, 128), size)],
                left.at[slot],
                left_sem.at[slot],
            ),
            pltpu.make_async_copy(
                summed.at[along, pl.ds(pl.multiple_of(across, 128), band_cols)],
                right.at[slot],
                right_sem.at[slot],
            ),
        )

    def start(copies):
        for copy in copies:
            copy.start()

    def multiply(k):
        def slab(n, carry):
            slot = lax.rem(n, 2)
            pl.when(n + 1 < slabs)(lambda: start(fetch(k, n + 1, 1 - slot)))
            pl.when((n + 1 == slabs) & (k + 1 < bands))(lambda: start(fetch(k + 1, 0, 1 - slot)))
            for copy in fetch(k, n, slot):
                copy.wait()
            turned[...] = left[slot].T * 2
            for c in range(0, band_cols, chunk):
                at = pl.ds(c, chunk)
                held[k, :, at] += jnp.dot(
                    turned[...], right[slot, :, at], preferred_element_type=jnp.float32
                )
            return carry

        held[k] = jnp.zeros(held.shape[1:], held.dtype)
        lax.fori_loop(0, slabs, slab, 0)

    def store(k):
        at = pl.ds(pl.multiple_of((k - shared) * size, size), size)
        across = pl.ds(pl.multiple_of(own_place, 128), band_cols)
        return pltpu.make_async_copy(held.at[k], out.at[at, across], out_sem.at[k])

    part_cols = band_cols // PARTS

    def part(ref, p):
        return ref.at[:, pl.ds(p * part_cols, part_cols)]

    def hop(side, k, p):
        return pltpu.make_async_remote_copy(
            src_ref=part(sends.at[side, lax.rem(k, 2)], p),
            dst_ref=part((ups, downs)[side].at[k], p),
            send_sem=(up_send, down_send)[side].at[k, p],
            recv_sem=(up_recv, down_recv)[side].at[k, p],
            device_id={"rep": (here + 1, here - 1)[side]},
            device_id_type=MESH,
        )

    def swap(k):
        return pltpu.make_async_remote_copy(
            src_ref=given.at[k],
            dst_ref=taken.at[k],
            send_sem=pair_send.at[k],
            recv_sem=pair_recv.at[k],
            device_id=twin,
            device_id_type=MESH,
        )

    def put(source, k, first):
        at = pl.ds(pl.multiple_of(jnp.where(first, 0, half) + k * size, size), size)

        @pl.when(low)
        def _():
            add_strips(square.at[at, :], source)

        @pl.when(jnp.logical_not(low))
        def _():
            def turn(n, carry):
                along = pl.ds(pl.multiple_of(n * 128, 128), 128)
                square[along, at] = source[:, along].astype(jnp.float32).T
                return carry

            lax.fori_loop(0, rows // 128, turn, 0)

    greet([], reps, [twin] if shared else [])
    start(fetch(0, 0, 0))
    multiply(0)

    def tick(t, carry):
        for p in range(PARTS):
            for side, depth in ((0, here), (1, mirror)):
                k = t - depth
                on = (k >= 0) & (k < bands) & (depth < reps - 1)
                pl.when(on & (k >= 2))(lambda: hop(side, k - 2, p).wait_send())
                buffer = part(sends.at[side, lax.rem(k + bands * reps * 2, 2)], p)

                @pl.when(on & (depth == 0))
                def _():
                    add_strips(buffer, part(held.at[k], p))
                    hop(side, k, p).start()

                @pl.when(on & (depth > 0))
                def _():
                    hop(side, k, p).wait_recv()
                    add_strips(buffer, part(held.at[k], p), part((ups, downs)[side].at[k], p))
                    hop(side, k, p).start()

        k = t - jnp.maximum(here, mirror)
        on = (k >= 0) & (k < bands)

        @pl.when(on & (here == 0))
        def _():
            for p in range(PARTS):
                hop(1, k, p).wait_recv()
            add_strips(held.at[k], held.at[k], downs.at[k])

        @pl.when(on & (mirror == 0))
        def _():
            for p in range(PARTS):
                hop(0, k, p).wait_recv()
            add_strips(held.at[k], held.at[k], ups.at[k])

        @pl.when(on & (here > 0) & (mirror > 0))
        def _():
            add_strips(held.at[k], held.at[k], ups.at[k], downs.at[k])

        pl.when(on & (k >= shared))(lambda: store(k).start())
        if shared:

            @pl.when(on & (k < shared))
            def _():
                add_strips(given.at[k], held.at[k])
                swap(k).start()
                put(held.at[k], k, low)

        pl.when(t + 1 < bands)(lambda: multiply(t + 1))
        return carry

    lax.fori_loop(0, bands + reps - 1, tick, 0)
    if shared:
        for k in range(shared):
            swap(k).wait()
            put(taken.at[k], k, jnp.logical_not(low))
        across = pl.ds(pl.multiple_of(twin_place, 128), rows)
        copy = pltpu.make_async_copy(square, out.at[:, across], square_sem)
        copy.start()
    for side, depth in ((0, here), (1, mirror)):
        for k in range(max(bands - 2, 0), bands):
            for p in range(PARTS):
                pl.when(depth < reps - 1)(lambda: hop(side, k, p).wait_send())

    def finish(k, carry):
        store(k).wait()
        return carry

    lax.fori_loop(shared, bands, finish, 0)
    if shared:
        copy.wait()


def total(summed, rows, cols):
    reps = lax.axis_size("rep")
    paired = cols == 2 * rows and lax.axis_size("row") == 2 * lax.axis_size("col")
    shared = BANDS // 2 if paired else 0
    bands, size = BANDS + shared, rows // BANDS
    band_cols = rows if paired else cols
    depth = summed.shape[0] // SLABS
    dma = pltpu.SemaphoreType.DMA
    shape = (bands, size, band_cols)
    extra = [
        pltpu.VMEM((shared, size, band_cols), jnp.bfloat16),
        pltpu.VMEM((shared, size, band_cols), jnp.bfloat16),
        pltpu.VMEM((rows, rows), jnp.float32),
        dma((max(shared, 1),)),
        dma((max(shared, 1),)),
        dma,
    ]
    return pl.pallas_call(
        functools.partial(total_kernel, reps, rows, cols, shared),
        out_shape=jax.ShapeDtypeStruct((rows, cols), jnp.float32),
        in_specs=[pl.BlockSpec(memory_space=pl.ANY)],
        out_specs=pl.BlockSpec(memory_space=pl.ANY),
        scratch_shapes=[
            pltpu.VMEM(shape, jnp.float32),
            pltpu.VMEM(shape, jnp.bfloat16),
            pltpu.VMEM(shape, jnp.bfloat16),
            pltpu.VMEM((2, 2) + shape[1:], jnp.bfloat16),
            pltpu.VMEM((2, depth, size), summed.dtype),
            pltpu.VMEM((2, depth, band_cols), summed.dtype),
            pltpu.VMEM((size, depth), summed.dtype),
            dma((2,)),
            dma((2,)),
        ]
        + [dma((bands,))]
        + [dma((bands, PARTS))] * 4
        + (extra if paired else []),
        compiler_params=pltpu.CompilerParams(
            collective_id=1, has_side_effects=True, vmem_limit_bytes=VMEM_LIMIT
        ),
    )(summed)


def shards(grad_parts, statistic):
    tile_rows, tile_cols = statistic.shape
    summed = collect(grad_parts[0])
    gram = 0.5 * total(summed, tile_rows, tile_cols)
    return (gram, 0.95 * statistic + 0.05 * gram)


def solution(mesh):
    return jax.shard_map(
        shards,
        mesh=mesh,
        in_specs=(P("rep", ("row", "col"), None), P("row", "col")),
        out_specs=(P("row", "col"), P("row", "col")),
        check_vma=False,
    )
```

profile of v0, /device:TPU:1, one launch (start us, length us, event | category | flops | bytes accessed | tf_op | source)
XLA Modules:
  0.0 663.0 jit_solution(2109609353554291035)
XLA Ops:
  0.6 377.5 %shard_map.41 = bf16[12,2,2,2,64,6144]{5,4,3,2,1,0:T(8,128)(2,1)} custom-call(bf16[2048,6144]{1,0:T(8,128)(2,1)} %bitcast.2), custom_call_target="tpu_custom_call" | custom-call | tf_op jit(solution)/shard_map/pallas_call | solution.py:269
  378.2 256.9 %shard_map.42 = f32[1536,3072]{1,0:T(8,128)} custom-call(bf16[6144,6144]{1,0:T(8,128)(2,1)} %bitcast.1.summed), custom_call_target="tpu_custom_call" | custom-call | tf_op jit(solution)/shard_map/pallas_call | solution.py:504
  635.1 27.9 %multiply_add_fusion = (f32[1536,3072]{1,0:T(8,128)}, f32[1536,3072]{1,0:T(8,128)}) fusion(f32[1536,3072]{1,0:T(8,128)} %shard_map.42, f32[1536,3072]{1,0:T(8,128)} %param.3), kind=kLoop, calls=%fused_computation | loop fusion | flops 18874368 | bytes 75497472 | tf_op jit(solution)/shard_map/add | solution.py:533
where the time goes:
time: 664 us; the launch traced here: 663 us
  Pallas kernels  634 us (95%)
  other arithmetic  27.9 us (4%)
    pallas_call x1, Pallas kernels, collect(): pl.pallas_call(functools.partial(collect_kernel, reps, bits, orders), out...  378 us
    pallas_call x1, Pallas kernels, total(): pl.pallas_call(functools.partial(total_kernel, reps, rows, cols, shared),...  257 us
    add x1, other arithmetic, shards(): return (gram, 0.95 * statistic + 0.05 * gram)  27.9 us

commit v1 on v0

--- a/solution.py
+++ b/solution.py
@@ -11,6 +11,7 @@
 MIDDLE = 4
 BANDS = 6
 PARTS = 2
+LAG = 3
 SLABS = 4
 CHUNK = 1536
 STRIP = 16
@@ -301,7 +302,11 @@
     mirror = reps - 1 - here
     bands, size, band_cols = held.shape
     depth = left.shape[1]
+    end, middle, _ = plan(reps)
+    valid = middle * (summed.shape[0] // end)
     slabs = summed.shape[0] // depth
+    fewer = min(slabs, 2 * pl.cdiv(valid, 2 * depth))
+    slabs = jnp.where((here > 0) & (mirror > 0), fewer, slabs)
     chunk = min(CHUNK, band_cols)
     row, col = lax.axis_index("row"), lax.axis_index("col")
     if shared:
@@ -392,6 +397,10 @@
             device_id_type=MESH,
         )
 
+    def store_square():
+        across = pl.ds(pl.multiple_of(twin_place, 128), rows)
+        return pltpu.make_async_copy(square, out.at[:, across], square_sem)
+
     def put(source, k, first):
         at = pl.ds(pl.multiple_of(jnp.where(first, 0, half) + k * size, size), size)
 
@@ -459,17 +468,18 @@
                 swap(k).start()
                 put(held.at[k], k, low)
 
+            late = t - jnp.maximum(here, mirror) - LAG
+
+            @pl.when((late >= 0) & (late < shared))
+            def _():
+                swap(late).wait()
+                put(taken.at[late], late, jnp.logical_not(low))
+                pl.when(late == shared - 1)(lambda: store_square().start())
+
         pl.when(t + 1 < bands)(lambda: multiply(t + 1))
         return carry
 
     lax.fori_loop(0, bands + reps - 1, tick, 0)
-    if shared:
-        for k in range(shared):
-            swap(k).wait()
-            put(taken.at[k], k, jnp.logical_not(low))
-        across = pl.ds(pl.multiple_of(twin_place, 128), rows)
-        copy = pltpu.make_async_copy(square, out.at[:, across], square_sem)
-        copy.start()
     for side, depth in ((0, here), (1, mirror)):
         for k in range(max(bands - 2, 0), bands):
             for p in range(PARTS):
@@ -481,7 +491,7 @@
 
     lax.fori_loop(shared, bands, finish, 0)
     if shared:
-        copy.wait()
+        store_square().wait()
 
 
 def total(summed, rows, cols):

time: 664 us -> 658 us (level)
  Pallas kernels: 634 us -> 627 us
    pallas_call x1, Pallas kernels: 257 us -> 250 us  [total(): pl.pallas_call(functools.partial(total_kernel, reps, rows, cols, shared),...]
where the time goes in v1:
time: 658 us; the launch traced here: 656 us
  Pallas kernels  627 us (95%)
  other arithmetic  27.9 us (4%)
    pallas_call x1, Pallas kernels, collect(): pl.pallas_call(functools.partial(collect_kernel, reps, bits, orders), out...  378 us
    pallas_call x1, Pallas kernels, total(): pl.pallas_call(functools.partial(total_kernel, reps, rows, cols, shared),...  250 us
    add x1, other arithmetic, shards(): return (gram, 0.95 * statistic + 0.05 * gram)  27.9 us

profile of v1, /device:TPU:1, one launch (start us, length us, event | category | flops | bytes accessed | tf_op | source)
XLA Modules:
  0.0 655.5 jit_solution(8657314143986435456)
XLA Ops:
  0.6 377.5 %shard_map.41 = bf16[12,2,2,2,64,6144]{5,4,3,2,1,0:T(8,128)(2,1)} custom-call(bf16[2048,6144]{1,0:T(8,128)(2,1)} %bitcast.2), custom_call_target="tpu_custom_call" | custom-call | tf_op jit(solution)/shard_map/pallas_call | solution.py:270
  378.2 249.5 %shard_map.42 = f32[1536,3072]{1,0:T(8,128)} custom-call(bf16[6144,6144]{1,0:T(8,128)(2,1)} %bitcast.1.summed), custom_call_target="tpu_custom_call" | custom-call | tf_op jit(solution)/shard_map/pallas_call | solution.py:514
  627.7 27.9 %multiply_add_fusion = (f32[1536,3072]{1,0:T(8,128)}, f32[1536,3072]{1,0:T(8,128)}) fusion(f32[1536,3072]{1,0:T(8,128)} %shard_map.42, f32[1536,3072]{1,0:T(8,128)} %param.3), kind=kLoop, calls=%fused_computation | loop fusion | flops 18874368 | bytes 75497472 | tf_op jit(solution)/shard_map/add | solution.py:543
